TPU v7x, 512 devices: a whole 4x8x8 slice. The times are simulated.
512 devices in a mesh: grp: 8 (over y), blk: 64 (over z, x, core).
Axes of the slice: x: 4, y: 8, z: 8, core: 2. Of those that a mesh axis runs over, the one named last changes fastest.
Arguments:
- query_rows: bfloat16 [12288, 4096], P('blk', 'grp'), may hold values from -128 to 128
- key_rows: bfloat16 [12288, 512], P(('grp', 'blk')), may hold values from -6 to 6
- value_rows: bfloat16 [12288, 512], P(('grp', 'blk')), may hold values from -6 to 6
- span_ids: int32 [128], P('blk'), may hold values from 0 to 127, as said below
Outputs:
- attended: bfloat16 [12288, 4096], P('blk', 'grp')
Inputs may be any that keep to these rules, and one draw needn't show every extreme that they name: `span_ids`: A permutation of 0 to 127; each device of blk holds two entries, in device order.
All inputs are finite; a program needn't handle non-finite values.
Results may differ from a plain program's by a relative error of at most 0.0045.
Values may be sent and summed in bfloat16 or wider, within the bound.
No kernel may reach another device: no remote copies, remote signals or barrier semaphores. Data moves between devices by JAX's collectives and lax.ppermute only.
A program may use at most 64 MiB of HBM per device.

v0:
```python
import functools
import math

import jax
import jax.numpy as jnp
from jax import lax
from jax.experimental import pallas as pl
from jax.experimental.pallas import tpu as pltpu
from jax.sharding import Mesh
from jax.sharding import PartitionSpec as P


HEAD_DIM = 128
SPAN = 96
PIECE = 24
ROWS = 784
KEYS = 384
HEADS = 4
COLS = 2 * HEADS * SPAN
STATE = 144
TILE = 256
GROUP = 4
MASKED = -1e30
FACTOR = HEAD_DIM**-0.5 * math.log2(math.e)
AXES = ("kv", "pair", "z", "x", "core")
BLK = ("z", "x", "core")
F32 = jnp.float32
BF16 = jnp.bfloat16


def pack_kernel(key_ref, value_ref, out_ref):
    for head in range(4):
        lanes = slice(head * HEAD_DIM, (head + 1) * HEAD_DIM)
        for x in range(4):
            out_ref[head, x, 0:24, :] = key_ref[:, lanes]
            out_ref[head, x, 24:48, :] = value_ref[:, lanes]


def label_kernel(packed_ref, ids_ref, out_ref):
    own = jnp.concatenate([ids_ref[...]] * 4, axis=0).astype(BF16)
    out_ref[:, :, 0:48, :] = packed_ref[...]
    out_ref[:, :, 48:56, :] = jnp.broadcast_to(own[None, None], (4, 4, 8, HEAD_DIM))


def spread_kernel(routed_ref, out_ref):
    for k in range(4):
        for x in range(4):
            at = (k * 4 + x) * PIECE
            out_ref[0, at : at + PIECE, :] = routed_ref[k, x, 0:24, :]
            out_ref[0, KEYS + at : KEYS + at + PIECE, :] = routed_ref[k, x, 24:48, :]
    rows = []
    for k in range(4):
        ids = sum(routed_ref[k, x, 48:56, :].astype(F32) for x in range(4))
        rows += [ids[0:1], ids[0:1], ids[1:2], ids[1:2]]
    out_ref[0, 2 * KEYS : ROWS, :] = jnp.concatenate(rows, axis=0).astype(BF16)


def stack_kernel(own_ref, beyond_ref, ids_ref, out_ref):
    ids = jnp.concatenate([ids_ref[...]] * 8, axis=0).astype(BF16)
    for e in range(2):
        for k in range(2 * HEADS):
            h = k % HEADS
            source = own_ref if k < HEADS else beyond_ref
            out_ref[e, k * SPAN : (k + 1) * SPAN, :] = source[
                e * SPAN : (e + 1) * SPAN, h * HEAD_DIM : (h + 1) * HEAD_DIM
            ]
        out_ref[e, COLS : COLS + 16, :] = ids


def attend_kernel(halves, sets, has_state, last, *refs):
    refs = list(refs)
    q_refs = [refs.pop(0) for _ in sets]
    count = sum(halves)
    given = [refs.pop(0) for _ in halves]
    block = [(g, h, n == 1) for g, n in zip(given, halves) for h in range(n)]
    state_ref = refs.pop(0) if has_state else None
    out_ref, turned, masks, one_hot, *held = refs
    weights, held = held[2:], held[:2]
    keys = KEYS * count

    turned[128:144, :] = jnp.ones((16, keys), BF16)
    for b in range(count):
        turned[0:128, b * KEYS : (b + 1) * KEYS] = block[b][0][block[b][1], KEYS : 2 * KEYS, :].T
    spot = lax.broadcasted_iota(jnp.int32, (SPAN, HEAD_DIM), 0)
    mark = lax.broadcasted_iota(jnp.int32, (SPAN, HEAD_DIM), 1)
    spike = jnp.where(spot == mark, 1.0, 0.0).astype(BF16)
    for k in range(2 * HEADS):
        one_hot[k * SPAN : (k + 1) * SPAN, :] = spike

    lane = lax.broadcasted_iota(jnp.int32, (PIECE, HEAD_DIM), 1)
    row = lax.broadcasted_iota(jnp.int32, (PIECE, HEAD_DIM), 0)
    ahead = (row - lane).astype(F32)
    here = ahead + (lax.axis_index("core") * PIECE).astype(F32)

    def mask(s):
        query_row = q_refs[s // 2][s % 2, COLS : COLS + 16, :].astype(F32)[s % 2 : s % 2 + 1]
        for b in range(count):
            ref, h, own = block[b]
            begin = here if own else ahead + float(h * PIECE)
            places = ref[h, 2 * KEYS : ROWS, :].astype(F32)
            limits = (query_row - places) * float(SPAN)
            for i in range(0, 16, 2):
                pieces = [
                    jnp.where(
                        begin + float(j % 2 * 2 * PIECE)
                        > jnp.broadcast_to(limits[j : j + 1], ahead.shape),
                        MASKED,
                        0.0,
                    )
                    for j in (i, i + 1)
                ]
                at = b * KEYS + i * PIECE
                masks[s, at : at + 2 * PIECE, :] = jnp.concatenate(pieces, axis=0).astype(BF16)

    flip = (((1,), (1,)), ((), ()))
    tiles = [(s, t) for s in range(2 * len(sets)) for t in range(COLS // TILE)]

    def score(i):
        s, t = tiles[i]
        if t == 0:
            mask(s)
        cols = slice(t * TILE, (t + 1) * TILE)
        right = jnp.concatenate([q_refs[s // 2][s % 2, cols, :], one_hot[cols, :]], axis=1)
        best = None
        for b in range(count):
            rows = slice(b * KEYS, (b + 1) * KEYS)
            left = jnp.concatenate([block[b][0][block[b][1], 0:KEYS, :], masks[s, rows, :]], axis=1)
            part = lax.dot_general(left, right, flip, preferred_element_type=F32)
            held[i % 2][rows, :] = part
            peak = jnp.max(part.reshape(KEYS // (8 * GROUP), 8 * GROUP, TILE), axis=0)
            best = peak if best is None else jnp.maximum(best, peak)
            yield best

    for best in score(0):
        pass
    for i, (s, t) in enumerate(tiles):
        cols = slice(t * TILE, (t + 1) * TILE)
        top = jnp.max(best, axis=0, keepdims=True)
        if has_state:
            at = 2 * sets[0] + s
            before = state_ref[at, 136:137, cols]
            top = jnp.maximum(before, top)
        ahead_scores = score(i + 1) if i + 1 < len(tiles) else iter([None] * count)
        for b in range(count):
            rows = slice(b * KEYS, (b + 1) * KEYS)
            weights[i % 2][rows, :] = jnp.exp2((held[i % 2][rows, :] - top) * FACTOR).astype(BF16)
            best = next(ahead_scores)
        sums = jnp.dot(turned[...], weights[i % 2][...], preferred_element_type=F32)[0:136]
        if has_state:
            sums = sums + state_ref[at, 0:136, cols] * jnp.exp2((before - top) * FACTOR)
        if last:
            pack_state(out_ref, (s,), cols, sums[0:128], sums[128:129], top)
        else:
            out_ref[s, 0:136, cols] = sums
            out_ref[s, 136:144, cols] = jnp.broadcast_to(top, (8, TILE))


def pack_state(out_ref, lead, cols, weighted, total, top):
    out_ref[(*lead, slice(0, 128), cols)] = weighted.astype(BF16)
    width = top.shape[1]
    line = lax.broadcasted_iota(jnp.int32, (16, width), 0)
    stats = jnp.zeros((16, width), F32)
    for base, value in ((0, top), (3, total)):
        for k in range(3):
            part = value.astype(BF16).astype(F32)
            value = value - part
            stats = jnp.where(line == base + k, jnp.broadcast_to(part, stats.shape), stats)
    out_ref[(*lead, slice(128, 144), cols)] = stats.astype(BF16)


def open_state(ref, lead, cols):
    stats = ref[(*lead, slice(128, 144), cols)].astype(F32)
    top = stats[0:1] + stats[1:2] + stats[2:3]
    total = stats[3:4] + stats[4:5] + stats[5:6]
    return ref[(*lead, slice(0, 128), cols)].astype(F32), total, top


def merge(mine, other):
    top = jnp.maximum(mine[2], other[2])
    a = jnp.exp2((mine[2] - top) * FACTOR)
    b = jnp.exp2((other[2] - top) * FACTOR)
    return mine[0] * a + other[0] * b, mine[1] * a + other[1] * b, top


def join_kernel(state_ref, come_ref, own_ref, out_ref):
    half = COLS // 2
    for e in range(2):
        for side in range(2):
            cols = slice(side * half, (side + 1) * half)
            mine = (state_ref[e, 0:128, cols], state_ref[e, 128:129, cols], state_ref[e, 136:137, cols])
            weighted, total, top = merge(mine, open_state(come_ref, (e,), cols))
            if side == 0:
                own_ref[e, 0:128, :] = weighted
                own_ref[e, 128:136, :] = jnp.broadcast_to(total, (8, half))
                own_ref[e, 136:144, :] = jnp.broadcast_to(top, (8, half))
            else:
                pack_state(out_ref, (e,), slice(0, half), weighted, total, top)


def finish_kernel(own_ref, come_ref, out_ref):
    half = COLS // 2
    everything = slice(0, half)
    for e in range(2):
        mine = (own_ref[e, 0:128, :], own_ref[e, 128:129, :], own_ref[e, 136:137, :])
        weighted, total, _ = merge(mine, open_state(come_ref, (e,), everything))
        mixed = (weighted / total).T.astype(BF16)
        for h in range(HEADS):
            out_ref[e * SPAN : (e + 1) * SPAN, h * HEAD_DIM : (h + 1) * HEAD_DIM] = mixed[
                h * SPAN : (h + 1) * SPAN
            ]


def attend(stacks, sets, blocks, state, last):
    halves = [block.shape[0] for block in blocks]
    count = sum(halves)
    steps = 2 * len(sets)
    keys = KEYS * count
    kernel = functools.partial(attend_kernel, halves, sets, state is not None, last)
    args = [stacks[s] for s in sets] + list(blocks)
    if state is not None:
        args.append(state)
    macs = steps * COLS * keys * (256 + STATE)
    return pl.pallas_call(
        kernel,
        out_shape=jax.ShapeDtypeStruct((steps, STATE, COLS), BF16 if last else F32),
        scratch_shapes=[
            pltpu.VMEM((STATE, keys), BF16),
            pltpu.VMEM((steps, keys, HEAD_DIM), BF16),
            pltpu.VMEM((COLS, HEAD_DIM), BF16),
            pltpu.VMEM((keys, TILE), F32),
            pltpu.VMEM((keys, TILE), F32),
            pltpu.VMEM((keys, TILE), BF16),
            pltpu.VMEM((keys, TILE), BF16),
        ],
        compiler_params=pltpu.CompilerParams(vmem_limit_bytes=14 * 1024 * 1024),
        cost_estimate=pl.CostEstimate(
            flops=4 * macs, bytes_accessed=2**20, transcendentals=steps * COLS * keys
        ),
    )(*args)


def call(kernel, out_shape, *args):
    return pl.pallas_call(
        kernel,
        out_shape=out_shape,
        compiler_params=pltpu.CompilerParams(vmem_limit_bytes=8 * 1024 * 1024),
        cost_estimate=pl.CostEstimate(flops=2**21, bytes_accessed=2**20, transcendentals=0),
    )(*args)


def around(value):
    zs = lax.axis_size("z")
    perm = []
    for z in range(zs):
        perm.append((2 * z, 2 * ((z - 1) % zs)))
        perm.append((2 * z + 1, 2 * ((z + 1) % zs) + 1))
    return lax.ppermute(value, ("z", "core"), perm)


def shifted(value, axis, step):
    size = lax.axis_size(axis)
    return lax.ppermute(value, axis, [(i, (i + step) % size) for i in range(size)])


def ids_to_keys(ids):
    size = {a: lax.axis_size(a) for a in AXES}

    def flat(g, z, x, core):
        return ((g * size["z"] + z) * size["x"] + x) * size["core"] + core

    perm = []
    for g in range(8):
        for z in range(8):
            for core in range(2):
                perm.append((flat(g ^ core, g, z // 2, z % 2), flat(g, z, z // 2, core)))
    return lax.ppermute(ids, AXES, perm)


def body(query_rows, key_rows, value_rows, span_ids):
    ids = jnp.broadcast_to(span_ids.astype(F32)[:, None], (2, HEAD_DIM))
    packed = call(
        pack_kernel, jax.ShapeDtypeStruct((4, 4, 48, HEAD_DIM), BF16), key_rows, value_rows
    )
    packed = call(
        label_kernel,
        jax.ShapeDtypeStruct((4, 4, 56, HEAD_DIM), BF16),
        packed,
        ids_to_keys(ids),
    ).reshape(16, 56, HEAD_DIM)
    routed = lax.all_to_all(packed, ("kv", "x"), 0, 0, tiled=True)
    routed = routed.reshape(4, 4, 56, HEAD_DIM)
    near = call(spread_kernel, jax.ShapeDtypeStruct((1, ROWS, HEAD_DIM), BF16), routed)
    chip = lax.all_gather(near, "core", axis=0, tiled=True)

    rings = [around(chip)]
    beyond = shifted(query_rows, "pair", 1)
    stack = call(
        stack_kernel,
        jax.ShapeDtypeStruct((2, COLS + 16, HEAD_DIM), BF16),
        query_rows,
        beyond,
        ids,
    )
    stacks = (stack, shifted(stack, "core", 1))
    for _ in range(2):
        rings.append(around(rings[-1]))
    far = around(lax.dynamic_slice_in_dim(rings[-1], lax.axis_index("core"), 1, 0))
    state = None
    for blocks in ([near, rings[0]], [rings[1]], [rings[2]]):
        state = attend(stacks, (0, 1), blocks, state, False)
    leaving = attend(stacks, (1,), [far], state, True)
    coming = shifted(leaving, "core", 1)
    mine = attend(stacks, (0,), [far], state, False)
    own, leaving = call(
        join_kernel,
        (
            jax.ShapeDtypeStruct((2, STATE, COLS // 2), F32),
            jax.ShapeDtypeStruct((2, STATE, COLS // 2), BF16),
        ),
        mine,
        coming,
    )
    coming = shifted(leaving, "pair", 1)
    return call(
        finish_kernel, jax.ShapeDtypeStruct((2 * SPAN, HEADS * HEAD_DIM), BF16), own, coming
    )


def solution(mesh):
    split = Mesh(mesh.devices.reshape(4, 2, 8, 4, 2), AXES)
    groups = ("kv", "pair")
    return jax.shard_map(
        body,
        mesh=split,
        in_specs=(P(BLK, groups), P(groups + BLK, None), P(groups + BLK, None), P(BLK)),
        out_specs=P(BLK, groups),
        check_vma=False,
    )
```

profile of v0, /device:TPU:1, one launch (start us, length us, event | category | flops | bytes accessed | tf_op | source)
XLA Modules:
  0.0 96.6 jit_solution(873789130207168980)
XLA Ops:
  0.0 0.0 copy-start
  0.0 0.7 convert_element_type.3
  0.7 0.1 broadcast_in_dim.2.ids_ref
  0.8 5.4 %collective-permute-start.1 = (f32[2,128]{1,0:T(2,128)S(1)}, f32[2,128]{1,0:T(2,128)S(1)}, u32[]{:S(2)}, u32[]{:S(2)}) collective-permute-start(f32[2,128]{1,0:T(2,128)S(1)} %broadcast_in_dim.2.ids_ref), channel_id=1, source_target_pairs={{0,0},{64,1},{1,8},{65,9},{2,18},{66,19},{3,26},{67,27},{4,36},{68... | collective-permute-start | bytes 3080 | tf_op jit(solution)/shard_map/ppermute | solution.py:276
  6.1 0.0 copy-start.1
  6.2 0.7 copy-done.1
  6.9 0.0 copy-start.2
  6.9 0.7 copy-done.2
  7.7 0.0 collective-permute-done.1.ids_ref
  7.7 22.5 %all_to_all.5 = bf16[16,56,128]{2,1,0:T(8,128)(2,1)S(1)} all-to-all(bf16[16,56,128]{2,1,0:T(8,128)(2,1)S(1)} %bitcast.2), channel_id=1, replica_groups=mesh['kv'=4,'pair'=2,'z'=8,'x'=4,'core'=2] {'kv','x'}, dimensions={0} | all-to-all | bytes 458752 | tf_op jit(solution)/shard_map/all_to_all | solution.py:290
  30.3 5.2 %all_gather.3 = bf16[2,784,128]{2,1,0:T(8,128)(2,1)S(1)} all-gather(bf16[1,784,128]{2,1,0:T(8,128)(2,1)S(1)} %shard_map.49.refs_2_), channel_id=1, replica_groups=mesh['kv'=4,'pair'=2,'z'=8,'x'=4,'core'=2] {'core'}, dimensions={0}, use_global_device_ids=true | all-gather | bytes 602112 | tf_op jit(solution)/shard_map/all_gather | solution.py:293
  35.4 1.9 %collective-permute-start.2 = (bf16[2,784,128]{2,1,0:T(8,128)(2,1)S(1)}, bf16[2,784,128]{2,1,0:T(8,128)(2,1)S(1)}, u32[]{:S(2)}, u32[]{:S(2)}) collective-permute-start(bf16[2,784,128]{2,1,0:T(8,128)(2,1)S(1)} %all_gather.3), channel_id=1, source_target_pairs={{0,56},{1,9},{8,0},{9,17},{16,8},{17,25},{24,16},{25,33},{32,24},{... | collective-permute-start | bytes 1204232 | tf_op jit(solution)/shard_map/ppermute | solution.py:257
  37.4 0.0 copy-done
  37.4 2.5 %collective-permute-start = (bf16[192,512]{1,0:T(8,128)(2,1)S(1)}, bf16[192,512]{1,0:T(8,128)(2,1)S(1)}, u32[]{:S(2)}, u32[]{:S(2)}) collective-permute-start(bf16[192,512]{1,0:T(8,128)(2,1)S(1)} %copy-done), channel_id=1, source_target_pairs={{0,64},{64,0},{1,65},{65,1},{2,66},{66,2},{3,67},{67,3},{4,68},{68... | collective-permute-start | bytes 589832 | tf_op jit(solution)/shard_map/ppermute | solution.py:262
  39.9 8.2 %collective-permute-done.2.refs_3_ = bf16[2,784,128]{2,1,0:T(8,128)(2,1)S(1)} collective-permute-done((bf16[2,784,128]{2,1,0:T(8,128)(2,1)S(1)}, bf16[2,784,128]{2,1,0:T(8,128)(2,1)S(1)}, u32[]{:S(2)}, u32[]{:S(2)}) %collective-permute-start.2) | collective-permute-done | bytes 401440 | tf_op jit(solution)/shard_map/ppermute | solution.py:257
  48.1 1.9 %collective-permute-start.3 = (bf16[2,784,128]{2,1,0:T(8,128)(2,1)S(1)}, bf16[2,784,128]{2,1,0:T(8,128)(2,1)S(1)}, u32[]{:S(2)}, u32[]{:S(2)}) collective-permute-start(bf16[2,784,128]{2,1,0:T(8,128)(2,1)S(1)} %collective-permute-done.2.refs_3_), channel_id=1, source_target_pairs={{0,56},{1,9},{8,0},{9,17},{16,8},{17,25},{24,16},{25,33},{32,24},{... | collective-permute-start | bytes 1204232 | tf_op jit(solution)/shard_map/ppermute | solution.py:257
  50.0 0.0 collective-permute-done.beyond_ref
  50.0 0.1 shard_map.46.refs_0_
  50.1 6.4 %collective-permute-start.6 = (bf16[2,784,128]{2,1,0:T(8,128)(2,1)S(1)}, bf16[2,784,128]{2,1,0:T(8,128)(2,1)S(1)}, u32[]{:S(2)}, u32[]{:S(2)}) collective-permute-start(bf16[2,784,128]{2,1,0:T(8,128)(2,1)S(1)} %shard_map.46.refs_0_), channel_id=1, source_target_pairs={{0,1},{1,0},{2,3},{3,2},{4,5},{5,4},{6,7},{7,6},{8,9},{9,8},{10,11... | collective-permute-start | bytes 1204232 | tf_op jit(solution)/shard_map/ppermute | solution.py:262
  56.5 1.4 %collective-permute-done.3.refs_2_ = bf16[2,784,128]{2,1,0:T(8,128)(2,1)S(1)} collective-permute-done((bf16[2,784,128]{2,1,0:T(8,128)(2,1)S(1)}, bf16[2,784,128]{2,1,0:T(8,128)(2,1)S(1)}, u32[]{:S(2)}, u32[]{:S(2)}) %collective-permute-start.3) | collective-permute-done | bytes 401440 | tf_op jit(solution)/shard_map/ppermute | solution.py:257
  57.9 1.9 %collective-permute-start.4 = (bf16[2,784,128]{2,1,0:T(8,128)(2,1)S(1)}, bf16[2,784,128]{2,1,0:T(8,128)(2,1)S(1)}, u32[]{:S(2)}, u32[]{:S(2)}) collective-permute-start(bf16[2,784,128]{2,1,0:T(8,128)(2,1)S(1)} %collective-permute-done.3.refs_2_), channel_id=1, source_target_pairs={{0,56},{1,9},{8,0},{9,17},{16,8},{17,25},{24,16},{25,33},{32,24},{... | collective-permute-start | bytes 1204232 | tf_op jit(solution)/shard_map/ppermute | solution.py:257
  59.8 0.0 collective-permute-done.6.refs_1_.refs_0_
  59.8 5.4 %shard_map.50.refs_3_ = f32[4,144,768]{2,1,0:T(8,128)S(1)} custom-call(bf16[2,784,128]{2,1,0:T(8,128)(2,1)S(1)} %shard_map.46.refs_0_, bf16[2,784,128]{2,1,0:T(8,128)(2,1)S(1)} %collective-permute-done.6.refs_1_.refs_0_, bf16[1,784,128]{2,1,0:T(8,128)(2,1)S(1)} %shard_map.49.refs_2_, bf16[2,784,128]{2,1,0:T(8,128)(2,1)S(1)} %collective-permute-done.2.refs_3_), custom_call_target="tpu_custom_call" | custom-call | flops 5662310400 | bytes 1048576 | tf_op jit(solution)/shard_map/pallas_call | solution.py:223
  65.2 4.0 %shard_map.51.refs_3_ = f32[4,144,768]{2,1,0:T(8,128)S(1)} custom-call(bf16[2,784,128]{2,1,0:T(8,128)(2,1)S(1)} %shard_map.46.refs_0_, bf16[2,784,128]{2,1,0:T(8,128)(2,1)S(1)} %collective-permute-done.6.refs_1_.refs_0_, bf16[2,784,128]{2,1,0:T(8,128)(2,1)S(1)} %collective-permute-done.3.refs_2_, f32[4,144,768]{2,1,0:T(8,128)S(1)} %shard_map.50.refs_3_), custom_call_target="tpu_custom_call" | custom-call | flops 3774873600 | bytes 1048576 | tf_op jit(solution)/shard_map/pallas_call | solution.py:223
  69.3 0.0 collective-permute-done.4.refs_2_
  69.3 2.1 %collective-permute-start.5 = (bf16[1,784,128]{2,1,0:T(8,128)(2,1)S(1)}, bf16[1,784,128]{2,1,0:T(8,128)(2,1)S(1)}, u32[]{:S(2)}, u32[]{:S(2)}) collective-permute-start(bf16[1,784,128]{2,1,0:T(8,128)(2,1)S(1)} %constant_dynamic-slice_fusion), channel_id=1, source_target_pairs={{0,56},{1,9},{8,0},{9,17},{16,8},{17,25},{24,16},{25,33},{32,24},{... | collective-permute-start | bytes 602120 | tf_op jit(solution)/shard_map/ppermute | solution.py:257
  71.4 4.0 %shard_map.52.refs_2_ = f32[4,144,768]{2,1,0:T(8,128)S(1)} custom-call(bf16[2,784,128]{2,1,0:T(8,128)(2,1)S(1)} %shard_map.46.refs_0_, bf16[2,784,128]{2,1,0:T(8,128)(2,1)S(1)} %collective-permute-done.6.refs_1_.refs_0_, bf16[2,784,128]{2,1,0:T(8,128)(2,1)S(1)} %collective-permute-done.4.refs_2_, f32[4,144,768]{2,1,0:T(8,128)S(1)} %shard_map.51.refs_3_), custom_call_target="tpu_custom_call" | custom-call | flops 3774873600 | bytes 1048576 | tf_op jit(solution)/shard_map/pallas_call | solution.py:223
  75.4 1.6 %collective-permute-done.5.refs_1_ = bf16[1,784,128]{2,1,0:T(8,128)(2,1)S(1)} collective-permute-done((bf16[1,784,128]{2,1,0:T(8,128)(2,1)S(1)}, bf16[1,784,128]{2,1,0:T(8,128)(2,1)S(1)}, u32[]{:S(2)}, u32[]{:S(2)}) %collective-permute-start.5) | collective-permute-done | bytes 200736 | tf_op jit(solution)/shard_map/ppermute | solution.py:257
  77.0 1.2 %shard_map.54 = bf16[2,144,768]{2,1,0:T(8,128)(2,1)S(1)} custom-call(bf16[2,784,128]{2,1,0:T(8,128)(2,1)S(1)} %collective-permute-done.6.refs_1_.refs_0_, bf16[1,784,128]{2,1,0:T(8,128)(2,1)S(1)} %collective-permute-done.5.refs_1_, f32[4,144,768]{2,1,0:T(8,128)S(1)} %shard_map.52.refs_2_), custom_call_target="tpu_custom_call" | custom-call | flops 943718400 | bytes 1048576 | tf_op jit(solution)/shard_map/pallas_call | solution.py:223
  78.2 7.5 %collective-permute-start.7 = (bf16[2,144,768]{2,1,0:T(8,128)(2,1)S(1)}, bf16[2,144,768]{2,1,0:T(8,128)(2,1)S(1)}, u32[]{:S(2)}, u32[]{:S(2)}) collective-permute-start(bf16[2,144,768]{2,1,0:T(8,128)(2,1)S(1)} %shard_map.54), channel_id=1, source_target_pairs={{0,1},{1,0},{2,3},{3,2},{4,5},{5,4},{6,7},{7,6},{8,9},{9,8},{10,11... | collective-permute-start | bytes 1327112 | tf_op jit(solution)/shard_map/ppermute | solution.py:262
  85.7 1.2 %shard_map.53.state_ref = f32[2,144,768]{2,1,0:T(8,128)S(1)} custom-call(bf16[2,784,128]{2,1,0:T(8,128)(2,1)S(1)} %shard_map.46.refs_0_, bf16[1,784,128]{2,1,0:T(8,128)(2,1)S(1)} %collective-permute-done.5.refs_1_, f32[4,144,768]{2,1,0:T(8,128)S(1)} %shard_map.52.refs_2_), custom_call_target="tpu_custom_call" | custom-call | flops 943718400 | bytes 1048576 | tf_op jit(solution)/shard_map/pallas_call | solution.py:223
  86.8 0.2 collective-permute-done.7.come_ref
  87.1 0.2 shard_map.55
  87.3 1.9 %collective-permute-start.8 = (bf16[2,144,384]{2,1,0:T(8,128)(2,1)S(1)}, bf16[2,144,384]{2,1,0:T(8,128)(2,1)S(1)}, u32[]{:S(2)}, u32[]{:S(2)}) collective-permute-start(bf16[2,144,384]{2,1,0:T(8,128)(2,1)S(1)} %get-tuple-element.8), channel_id=1, source_target_pairs={{0,64},{64,0},{1,65},{65,1},{2,66},{66,2},{3,67},{67,3},{4,68},{68... | collective-permute-start | bytes 663560 | tf_op jit(solution)/shard_map/ppermute | solution.py:262
  89.2 6.6 %collective-permute-done.8.come_ref = bf16[2,144,384]{2,1,0:T(8,128)(2,1)S(1)} collective-permute-done((bf16[2,144,384]{2,1,0:T(8,128)(2,1)S(1)}, bf16[2,144,384]{2,1,0:T(8,128)(2,1)S(1)}, u32[]{:S(2)}, u32[]{:S(2)}) %collective-permute-start.8) | collective-permute-done | bytes 221216 | tf_op jit(solution)/shard_map/ppermute | solution.py:262
  95.8 0.9 shard_map.56
  (4 shorter events, 0.1 us)
Async XLA Ops:
  0.0 37.4 %copy-start = (bf16[192,512]{1,0:T(8,128)(2,1)S(1)}, bf16[192,512]{1,0:T(8,128)(2,1)}, u32[]{:S(2)}) copy-start(bf16[192,512]{1,0:T(8,128)(2,1)} %own_ref.1) | copy-start | bytes 589828
  0.8 6.9 %collective-permute-start.1 = (f32[2,128]{1,0:T(2,128)S(1)}, f32[2,128]{1,0:T(2,128)S(1)}, u32[]{:S(2)}, u32[]{:S(2)}) collective-permute-start(f32[2,128]{1,0:T(2,128)S(1)} %broadcast_in_dim.2.ids_ref), channel_id=1, source_target_pairs={{0,0},{64,1},{1,8},{65,9},{2,18},{66,19},{3,26},{67,27},{4,36},{68... | collective-permute-start | bytes 3080 | tf_op jit(solution)/shard_map/ppermute | solution.py:276
  6.1 0.7 copy-start.1
  6.9 0.7 copy-start.2
  35.4 12.7 %collective-permute-start.2 = (bf16[2,784,128]{2,1,0:T(8,128)(2,1)S(1)}, bf16[2,784,128]{2,1,0:T(8,128)(2,1)S(1)}, u32[]{:S(2)}, u32[]{:S(2)}) collective-permute-start(bf16[2,784,128]{2,1,0:T(8,128)(2,1)S(1)} %all_gather.3), channel_id=1, source_target_pairs={{0,56},{1,9},{8,0},{9,17},{16,8},{17,25},{24,16},{25,33},{32,24},{... | collective-permute-start | bytes 1204232 | tf_op jit(solution)/shard_map/ppermute | solution.py:257
  37.4 12.7 %collective-permute-start = (bf16[192,512]{1,0:T(8,128)(2,1)S(1)}, bf16[192,512]{1,0:T(8,128)(2,1)S(1)}, u32[]{:S(2)}, u32[]{:S(2)}) collective-permute-start(bf16[192,512]{1,0:T(8,128)(2,1)S(1)} %copy-done), channel_id=1, source_target_pairs={{0,64},{64,0},{1,65},{65,1},{2,66},{66,2},{3,67},{67,3},{4,68},{68... | collective-permute-start | bytes 589832 | tf_op jit(solution)/shard_map/ppermute | solution.py:262
  48.1 9.8 %collective-permute-start.3 = (bf16[2,784,128]{2,1,0:T(8,128)(2,1)S(1)}, bf16[2,784,128]{2,1,0:T(8,128)(2,1)S(1)}, u32[]{:S(2)}, u32[]{:S(2)}) collective-permute-start(bf16[2,784,128]{2,1,0:T(8,128)(2,1)S(1)} %collective-permute-done.2.refs_3_), channel_id=1, source_target_pairs={{0,56},{1,9},{8,0},{9,17},{16,8},{17,25},{24,16},{25,33},{32,24},{... | collective-permute-start | bytes 1204232 | tf_op jit(solution)/shard_map/ppermute | solution.py:257
  50.1 9.7 %collective-permute-start.6 = (bf16[2,784,128]{2,1,0:T(8,128)(2,1)S(1)}, bf16[2,784,128]{2,1,0:T(8,128)(2,1)S(1)}, u32[]{:S(2)}, u32[]{:S(2)}) collective-permute-start(bf16[2,784,128]{2,1,0:T(8,128)(2,1)S(1)} %shard_map.46.refs_0_), channel_id=1, source_target_pairs={{0,1},{1,0},{2,3},{3,2},{4,5},{5,4},{6,7},{7,6},{8,9},{9,8},{10,11... | collective-permute-start | bytes 1204232 | tf_op jit(solution)/shard_map/ppermute | solution.py:262
  57.9 11.3 %collective-permute-start.4 = (bf16[2,784,128]{2,1,0:T(8,128)(2,1)S(1)}, bf16[2,784,128]{2,1,0:T(8,128)(2,1)S(1)}, u32[]{:S(2)}, u32[]{:S(2)}) collective-permute-start(bf16[2,784,128]{2,1,0:T(8,128)(2,1)S(1)} %collective-permute-done.3.refs_2_), channel_id=1, source_target_pairs={{0,56},{1,9},{8,0},{9,17},{16,8},{17,25},{24,16},{25,33},{32,24},{... | collective-permute-start | bytes 1204232 | tf_op jit(solution)/shard_map/ppermute | solution.py:257
  69.3 7.7 %collective-permute-start.5 = (bf16[1,784,128]{2,1,0:T(8,128)(2,1)S(1)}, bf16[1,784,128]{2,1,0:T(8,128)(2,1)S(1)}, u32[]{:S(2)}, u32[]{:S(2)}) collective-permute-start(bf16[1,784,128]{2,1,0:T(8,128)(2,1)S(1)} %constant_dynamic-slice_fusion), channel_id=1, source_target_pairs={{0,56},{1,9},{8,0},{9,17},{16,8},{17,25},{24,16},{25,33},{32,24},{... | collective-permute-start | bytes 602120 | tf_op jit(solution)/shard_map/ppermute | solution.py:257
  78.2 8.9 %collective-permute-start.7 = (bf16[2,144,768]{2,1,0:T(8,128)(2,1)S(1)}, bf16[2,144,768]{2,1,0:T(8,128)(2,1)S(1)}, u32[]{:S(2)}, u32[]{:S(2)}) collective-permute-start(bf16[2,144,768]{2,1,0:T(8,128)(2,1)S(1)} %shard_map.54), channel_id=1, source_target_pairs={{0,1},{1,0},{2,3},{3,2},{4,5},{5,4},{6,7},{7,6},{8,9},{9,8},{10,11... | collective-permute-start | bytes 1327112 | tf_op jit(solution)/shard_map/ppermute | solution.py:262
  87.3 8.5 %collective-permute-start.8 = (bf16[2,144,384]{2,1,0:T(8,128)(2,1)S(1)}, bf16[2,144,384]{2,1,0:T(8,128)(2,1)S(1)}, u32[]{:S(2)}, u32[]{:S(2)}) collective-permute-start(bf16[2,144,384]{2,1,0:T(8,128)(2,1)S(1)} %get-tuple-element.8), channel_id=1, source_target_pairs={{0,64},{64,0},{1,65},{65,1},{2,66},{66,2},{3,67},{67,3},{4,68},{68... | collective-permute-start | bytes 663560 | tf_op jit(solution)/shard_map/ppermute | solution.py:262
where the time goes:
time: 97.1 us; the launch traced here: 96.6 us
  starting transfers between devices  31.4 us (32%)
  blocking collectives  27.7 us (29%)
  waiting for transfers between devices  18 us (19%)
  Pallas kernels  17 us (18%)
  local copies, waits for them, and re-layouts  1.57 us (2%)
    all_to_all x1, blocking collectives, body(): routed = lax.all_to_all(packed, ('kv', 'x'), 0, 0, tiled=True)  22.5 us
    ppermute x4, starting transfers between devices, shifted(): lax.ppermute(value, axis, [(i, (i + step) % size) for i in range(size)])  18.3 us
    pallas_call x5, Pallas kernels, attend(): pl.pallas_call(kernel, out_shape=jax.ShapeDtypeStruct((steps, STATE, COLS...  15.8 us
    ppermute x4, waiting for transfers between devices, around(): return lax.ppermute(value, ('z', 'core'), perm)  11.2 us
    ppermute x4, starting transfers between devices, around(): return lax.ppermute(value, ('z', 'core'), perm)  7.83 us
    ppermute x4, waiting for transfers between devices, shifted(): lax.ppermute(value, axis, [(i, (i + step) % size) for i in range(size)])  6.8 us
    ppermute x1, starting transfers between devices, ids_to_keys(): return lax.ppermute(ids, AXES, perm)  5.37 us
    all_gather x1, blocking collectives, body(): chip = lax.all_gather(near, 'core', axis=0, tiled=True)  5.19 us
  transfers between devices with their start and end apart: 9, of which 5 were waited for; matrix products, arithmetic and copies ran while one was open for 0% of the time, Pallas kernels for 15%

commit v1 on v0

--- a/solution.py
+++ b/solution.py
@@ -28,18 +28,14 @@
 BF16 = jnp.bfloat16
 
 
-def pack_kernel(key_ref, value_ref, out_ref):
+def pack_kernel(key_ref, value_ref, ids_ref, out_ref):
+    own = jnp.concatenate([ids_ref[...]] * 4, axis=0).astype(BF16)
     for head in range(4):
         lanes = slice(head * HEAD_DIM, (head + 1) * HEAD_DIM)
         for x in range(4):
             out_ref[head, x, 0:24, :] = key_ref[:, lanes]
             out_ref[head, x, 24:48, :] = value_ref[:, lanes]
-
-
-def label_kernel(packed_ref, ids_ref, out_ref):
-    own = jnp.concatenate([ids_ref[...]] * 4, axis=0).astype(BF16)
-    out_ref[:, :, 0:48, :] = packed_ref[...]
-    out_ref[:, :, 48:56, :] = jnp.broadcast_to(own[None, None], (4, 4, 8, HEAD_DIM))
+            out_ref[head, x, 48:56, :] = own
 
 
 def spread_kernel(routed_ref, out_ref):
@@ -55,16 +51,30 @@
     out_ref[0, 2 * KEYS : ROWS, :] = jnp.concatenate(rows, axis=0).astype(BF16)
 
 
+def reorder(source, out_ref, first):
+    for e in range(2):
+        for h in range(HEADS):
+            at = first + h * SPAN
+            out_ref[e, at : at + SPAN, :] = source[
+                e * SPAN : (e + 1) * SPAN, h * HEAD_DIM : (h + 1) * HEAD_DIM
+            ]
+
+
+def reorder_kernel(source_ref, out_ref):
+    reorder(source_ref, out_ref, 0)
+
+
 def stack_kernel(own_ref, beyond_ref, ids_ref, out_ref):
     ids = jnp.concatenate([ids_ref[...]] * 8, axis=0).astype(BF16)
+    reorder(beyond_ref, out_ref, COLS // 2)
     for e in range(2):
-        for k in range(2 * HEADS):
-            h = k % HEADS
-            source = own_ref if k < HEADS else beyond_ref
-            out_ref[e, k * SPAN : (k + 1) * SPAN, :] = source[
-                e * SPAN : (e + 1) * SPAN, h * HEAD_DIM : (h + 1) * HEAD_DIM
-            ]
+        out_ref[e, 0 : COLS // 2, :] = own_ref[e]
         out_ref[e, COLS : COLS + 16, :] = ids
+
+
+def take_kernel(pair_ref, out_ref):
+    first = lax.axis_index("core") == 0
+    out_ref[0] = jnp.where(first, pair_ref[0], pair_ref[1])
 
 
 def attend_kernel(halves, sets, has_state, last, *refs):
@@ -278,14 +288,13 @@
 
 def body(query_rows, key_rows, value_rows, span_ids):
     ids = jnp.broadcast_to(span_ids.astype(F32)[:, None], (2, HEAD_DIM))
+    places = ids_to_keys(ids)
     packed = call(
-        pack_kernel, jax.ShapeDtypeStruct((4, 4, 48, HEAD_DIM), BF16), key_rows, value_rows
-    )
-    packed = call(
-        label_kernel,
+        pack_kernel,
         jax.ShapeDtypeStruct((4, 4, 56, HEAD_DIM), BF16),
-        packed,
-        ids_to_keys(ids),
+        key_rows,
+        value_rows,
+        places,
     ).reshape(16, 56, HEAD_DIM)
     routed = lax.all_to_all(packed, ("kv", "x"), 0, 0, tiled=True)
     routed = routed.reshape(4, 4, 56, HEAD_DIM)
@@ -294,17 +303,20 @@
 
     rings = [around(chip)]
     beyond = shifted(query_rows, "pair", 1)
+    own = call(
+        reorder_kernel, jax.ShapeDtypeStruct((2, COLS // 2, HEAD_DIM), BF16), query_rows
+    )
     stack = call(
         stack_kernel,
         jax.ShapeDtypeStruct((2, COLS + 16, HEAD_DIM), BF16),
-        query_rows,
+        own,
         beyond,
         ids,
     )
     stacks = (stack, shifted(stack, "core", 1))
     for _ in range(2):
         rings.append(around(rings[-1]))
-    far = around(lax.dynamic_slice_in_dim(rings[-1], lax.axis_index("core"), 1, 0))
+    far = around(call(take_kernel, jax.ShapeDtypeStruct(near.shape, BF16), rings[2]))
     state = None
     for blocks in ([near, rings[0]], [rings[1]], [rings[2]]):
         state = attend(stacks, (0, 1), blocks, state, False)

time: 97.1 us -> 98.6 us (1.015)
  transfers between devices with their start and end apart: 9 -> 9, of which waited for: 5 -> 6; matrix products, arithmetic and copies ran while one was open for 0% -> 0% of each run, Pallas kernels for 15% -> 15%
where the time goes in v1:
time: 98.6 us; the launch traced here: 98.1 us
  starting transfers between devices  31.4 us (32%)
  blocking collectives  28.5 us (29%)
  waiting for transfers between devices  18.8 us (19%)
  Pallas kernels  16.9 us (17%)
  local copies, waits for them, and re-layouts  1.55 us (2%)
    all_to_all x1, blocking collectives, body(): routed = lax.all_to_all(packed, ('kv', 'x'), 0, 0, tiled=True)  23.3 us
    ppermute x4, starting transfers between devices, shifted(): lax.ppermute(value, axis, [(i, (i + step) % size) for i in range(size)])  18.3 us
    pallas_call x5, Pallas kernels, attend(): pl.pallas_call(kernel, out_shape=jax.ShapeDtypeStruct((steps, STATE, COLS...  15.7 us
    ppermute x4, waiting for transfers between devices, around(): return lax.ppermute(value, ('z', 'core'), perm)  11.3 us
    ppermute x4, starting transfers between devices, around(): return lax.ppermute(value, ('z', 'core'), perm)  7.83 us
    ppermute x4, waiting for transfers between devices, shifted(): lax.ppermute(value, axis, [(i, (i + step) % size) for i in range(size)])  6.8 us
    ppermute x1, starting transfers between devices, ids_to_keys(): return lax.ppermute(ids, AXES, perm)  5.37 us
    all_gather x1, blocking collectives, body(): chip = lax.all_gather(near, 'core', axis=0, tiled=True)  5.19 us
  transfers between devices with their start and end apart: 9, of which 6 were waited for; matrix products, arithmetic and copies ran while one was open for 0% of the time, Pallas kernels for 15%

profile of v1, /device:TPU:1, one launch (start us, length us, event | category | flops | bytes accessed | tf_op | source)
XLA Modules:
  0.0 98.1 jit_solution(6630370990589013620)
XLA Ops:
  0.0 0.0 copy-start
  0.0 0.7 convert_element_type.3
  0.7 0.1 broadcast_in_dim.2.ids_ref
  0.8 5.4 %collective-permute-start.1 = (f32[2,128]{1,0:T(2,128)S(1)}, f32[2,128]{1,0:T(2,128)S(1)}, u32[]{:S(2)}, u32[]{:S(2)}) collective-permute-start(f32[2,128]{1,0:T(2,128)S(1)} %broadcast_in_dim.2.ids_ref), channel_id=1, source_target_pairs={{0,0},{64,1},{1,8},{65,9},{2,18},{66,19},{3,26},{67,27},{4,36},{68... | collective-permute-start | bytes 3080 | tf_op jit(solution)/shard_map/ppermute | solution.py:286
  6.1 0.7 collective-permute-done.1.ids_ref
  6.9 0.0 copy-start.1
  6.9 0.7 copy-done.1
  7.6 0.0 copy-start.2
  7.6 0.7 copy-done.2
  8.4 23.3 %all_to_all.5 = bf16[16,56,128]{2,1,0:T(8,128)(2,1)S(1)} all-to-all(bf16[16,56,128]{2,1,0:T(8,128)(2,1)S(1)} %bitcast.2), channel_id=1, replica_groups=mesh['kv'=4,'pair'=2,'z'=8,'x'=4,'core'=2] {'kv','x'}, dimensions={0} | all-to-all | bytes 458752 | tf_op jit(solution)/shard_map/all_to_all | solution.py:299
  31.7 5.2 %all_gather.3 = bf16[2,784,128]{2,1,0:T(8,128)(2,1)S(1)} all-gather(bf16[1,784,128]{2,1,0:T(8,128)(2,1)S(1)} %shard_map.49.refs_2_), channel_id=1, replica_groups=mesh['kv'=4,'pair'=2,'z'=8,'x'=4,'core'=2] {'core'}, dimensions={0}, use_global_device_ids=true | all-gather | bytes 602112 | tf_op jit(solution)/shard_map/all_gather | solution.py:302
  36.9 1.9 %collective-permute-start.2 = (bf16[2,784,128]{2,1,0:T(8,128)(2,1)S(1)}, bf16[2,784,128]{2,1,0:T(8,128)(2,1)S(1)}, u32[]{:S(2)}, u32[]{:S(2)}) collective-permute-start(bf16[2,784,128]{2,1,0:T(8,128)(2,1)S(1)} %all_gather.3), channel_id=1, source_target_pairs={{0,56},{1,9},{8,0},{9,17},{16,8},{17,25},{24,16},{25,33},{32,24},{... | collective-permute-start | bytes 1204232 | tf_op jit(solution)/shard_map/ppermute | solution.py:267
  38.8 0.0 copy-done
  38.9 2.5 %collective-permute-start = (bf16[192,512]{1,0:T(8,128)(2,1)S(1)}, bf16[192,512]{1,0:T(8,128)(2,1)S(1)}, u32[]{:S(2)}, u32[]{:S(2)}) collective-permute-start(bf16[192,512]{1,0:T(8,128)(2,1)S(1)} %copy-done), channel_id=1, source_target_pairs={{0,64},{64,0},{1,65},{65,1},{2,66},{66,2},{3,67},{67,3},{4,68},{68... | collective-permute-start | bytes 589832 | tf_op jit(solution)/shard_map/ppermute | solution.py:272
  41.4 8.2 %collective-permute-done.2.refs_3_ = bf16[2,784,128]{2,1,0:T(8,128)(2,1)S(1)} collective-permute-done((bf16[2,784,128]{2,1,0:T(8,128)(2,1)S(1)}, bf16[2,784,128]{2,1,0:T(8,128)(2,1)S(1)}, u32[]{:S(2)}, u32[]{:S(2)}) %collective-permute-start.2) | collective-permute-done | bytes 401440 | tf_op jit(solution)/shard_map/ppermute | solution.py:267
  49.6 1.9 %collective-permute-start.3 = (bf16[2,784,128]{2,1,0:T(8,128)(2,1)S(1)}, bf16[2,784,128]{2,1,0:T(8,128)(2,1)S(1)}, u32[]{:S(2)}, u32[]{:S(2)}) collective-permute-start(bf16[2,784,128]{2,1,0:T(8,128)(2,1)S(1)} %collective-permute-done.2.refs_3_), channel_id=1, source_target_pairs={{0,56},{1,9},{8,0},{9,17},{16,8},{17,25},{24,16},{25,33},{32,24},{... | collective-permute-start | bytes 1204232 | tf_op jit(solution)/shard_map/ppermute | solution.py:267
  51.5 0.0 collective-permute-done.beyond_ref
  51.5 0.1 shard_map.47.refs_0_
  51.6 6.4 %collective-permute-start.6 = (bf16[2,784,128]{2,1,0:T(8,128)(2,1)S(1)}, bf16[2,784,128]{2,1,0:T(8,128)(2,1)S(1)}, u32[]{:S(2)}, u32[]{:S(2)}) collective-permute-start(bf16[2,784,128]{2,1,0:T(8,128)(2,1)S(1)} %shard_map.47.refs_0_), channel_id=1, source_target_pairs={{0,1},{1,0},{2,3},{3,2},{4,5},{5,4},{6,7},{7,6},{8,9},{9,8},{10,11... | collective-permute-start | bytes 1204232 | tf_op jit(solution)/shard_map/ppermute | solution.py:272
  58.0 1.5 %collective-permute-done.3.refs_2_ = bf16[2,784,128]{2,1,0:T(8,128)(2,1)S(1)} collective-permute-done((bf16[2,784,128]{2,1,0:T(8,128)(2,1)S(1)}, bf16[2,784,128]{2,1,0:T(8,128)(2,1)S(1)}, u32[]{:S(2)}, u32[]{:S(2)}) %collective-permute-start.3) | collective-permute-done | bytes 401440 | tf_op jit(solution)/shard_map/ppermute | solution.py:267
  59.4 1.9 %collective-permute-start.4 = (bf16[2,784,128]{2,1,0:T(8,128)(2,1)S(1)}, bf16[2,784,128]{2,1,0:T(8,128)(2,1)S(1)}, u32[]{:S(2)}, u32[]{:S(2)}) collective-permute-start(bf16[2,784,128]{2,1,0:T(8,128)(2,1)S(1)} %collective-permute-done.3.refs_2_), channel_id=1, source_target_pairs={{0,56},{1,9},{8,0},{9,17},{16,8},{17,25},{24,16},{25,33},{32,24},{... | collective-permute-start | bytes 1204232 | tf_op jit(solution)/shard_map/ppermute | solution.py:267
  61.3 0.0 collective-permute-done.6.refs_1_.refs_0_
  61.3 5.4 %shard_map.51.refs_3_ = f32[4,144,768]{2,1,0:T(8,128)S(1)} custom-call(bf16[2,784,128]{2,1,0:T(8,128)(2,1)S(1)} %shard_map.47.refs_0_, bf16[2,784,128]{2,1,0:T(8,128)(2,1)S(1)} %collective-permute-done.6.refs_1_.refs_0_, bf16[1,784,128]{2,1,0:T(8,128)(2,1)S(1)} %shard_map.49.refs_2_, bf16[2,784,128]{2,1,0:T(8,128)(2,1)S(1)} %collective-permute-done.2.refs_3_), custom_call_target="tpu_custom_call" | custom-call | flops 5662310400 | bytes 1048576 | tf_op jit(solution)/shard_map/pallas_call | solution.py:233
  66.7 4.0 %shard_map.52.refs_3_ = f32[4,144,768]{2,1,0:T(8,128)S(1)} custom-call(bf16[2,784,128]{2,1,0:T(8,128)(2,1)S(1)} %shard_map.47.refs_0_, bf16[2,784,128]{2,1,0:T(8,128)(2,1)S(1)} %collective-permute-done.6.refs_1_.refs_0_, bf16[2,784,128]{2,1,0:T(8,128)(2,1)S(1)} %collective-permute-done.3.refs_2_, f32[4,144,768]{2,1,0:T(8,128)S(1)} %shard_map.51.refs_3_), custom_call_target="tpu_custom_call" | custom-call | flops 3774873600 | bytes 1048576 | tf_op jit(solution)/shard_map/pallas_call | solution.py:233
  70.7 0.0 collective-permute-done.4.pair_ref.refs_2_
  70.7 0.1 shard_map.50
  70.8 2.1 %collective-permute-start.5 = (bf16[1,784,128]{2,1,0:T(8,128)(2,1)S(1)}, bf16[1,784,128]{2,1,0:T(8,128)(2,1)S(1)}, u32[]{:S(2)}, u32[]{:S(2)}) collective-permute-start(bf16[1,784,128]{2,1,0:T(8,128)(2,1)S(1)} %shard_map.50), channel_id=1, source_target_pairs={{0,56},{1,9},{8,0},{9,17},{16,8},{17,25},{24,16},{25,33},{32,24},{... | collective-permute-start | bytes 602120 | tf_op jit(solution)/shard_map/ppermute | solution.py:267
  72.9 3.9 %shard_map.53.refs_2_ = f32[4,144,768]{2,1,0:T(8,128)S(1)} custom-call(bf16[2,784,128]{2,1,0:T(8,128)(2,1)S(1)} %shard_map.47.refs_0_, bf16[2,784,128]{2,1,0:T(8,128)(2,1)S(1)} %collective-permute-done.6.refs_1_.refs_0_, bf16[2,784,128]{2,1,0:T(8,128)(2,1)S(1)} %collective-permute-done.4.pair_ref.refs_2_, f32[4,144,768]{2,1,0:T(8,128)S(1)} %shard_map.52.refs_3_), custom_call_target="tpu_custom_call" | custom-call | flops 3774873600 | bytes 1048576 | tf_op jit(solution)/shard_map/pallas_call | solution.py:233
  76.8 1.6 %collective-permute-done.5.refs_1_ = bf16[1,784,128]{2,1,0:T(8,128)(2,1)S(1)} collective-permute-done((bf16[1,784,128]{2,1,0:T(8,128)(2,1)S(1)}, bf16[1,784,128]{2,1,0:T(8,128)(2,1)S(1)}, u32[]{:S(2)}, u32[]{:S(2)}) %collective-permute-start.5) | collective-permute-done | bytes 200736 | tf_op jit(solution)/shard_map/ppermute | solution.py:267
  78.5 1.2 %shard_map.55 = bf16[2,144,768]{2,1,0:T(8,128)(2,1)S(1)} custom-call(bf16[2,784,128]{2,1,0:T(8,128)(2,1)S(1)} %collective-permute-done.6.refs_1_.refs_0_, bf16[1,784,128]{2,1,0:T(8,128)(2,1)S(1)} %collective-permute-done.5.refs_1_, f32[4,144,768]{2,1,0:T(8,128)S(1)} %shard_map.53.refs_2_), custom_call_target="tpu_custom_call" | custom-call | flops 943718400 | bytes 1048576 | tf_op jit(solution)/shard_map/pallas_call | solution.py:233
  79.7 7.4 %collective-permute-start.7 = (bf16[2,144,768]{2,1,0:T(8,128)(2,1)S(1)}, bf16[2,144,768]{2,1,0:T(8,128)(2,1)S(1)}, u32[]{:S(2)}, u32[]{:S(2)}) collective-permute-start(bf16[2,144,768]{2,1,0:T(8,128)(2,1)S(1)} %shard_map.55), channel_id=1, source_target_pairs={{0,1},{1,0},{2,3},{3,2},{4,5},{5,4},{6,7},{7,6},{8,9},{9,8},{10,11... | collective-permute-start | bytes 1327112 | tf_op jit(solution)/shard_map/ppermute | solution.py:272
  87.1 1.2 %shard_map.54.state_ref = f32[2,144,768]{2,1,0:T(8,128)S(1)} custom-call(bf16[2,784,128]{2,1,0:T(8,128)(2,1)S(1)} %shard_map.47.refs_0_, bf16[1,784,128]{2,1,0:T(8,128)(2,1)S(1)} %collective-permute-done.5.refs_1_, f32[4,144,768]{2,1,0:T(8,128)S(1)} %shard_map.53.refs_2_), custom_call_target="tpu_custom_call" | custom-call | flops 943718400 | bytes 1048576 | tf_op jit(solution)/shard_map/pallas_call | solution.py:233
  88.3 0.2 collective-permute-done.7.come_ref
  88.5 0.2 shard_map.56
  88.7 1.9 %collective-permute-start.8 = (bf16[2,144,384]{2,1,0:T(8,128)(2,1)S(1)}, bf16[2,144,384]{2,1,0:T(8,128)(2,1)S(1)}, u32[]{:S(2)}, u32[]{:S(2)}) collective-permute-start(bf16[2,144,384]{2,1,0:T(8,128)(2,1)S(1)} %get-tuple-element.8), channel_id=1, source_target_pairs={{0,64},{64,0},{1,65},{65,1},{2,66},{66,2},{3,67},{67,3},{4,68},{68... | collective-permute-start | bytes 663560 | tf_op jit(solution)/shard_map/ppermute | solution.py:272
  90.7 6.6 %collective-permute-done.8.come_ref = bf16[2,144,384]{2,1,0:T(8,128)(2,1)S(1)} collective-permute-done((bf16[2,144,384]{2,1,0:T(8,128)(2,1)S(1)}, bf16[2,144,384]{2,1,0:T(8,128)(2,1)S(1)}, u32[]{:S(2)}, u32[]{:S(2)}) %collective-permute-start.8) | collective-permute-done | bytes 221216 | tf_op jit(solution)/shard_map/ppermute | solution.py:272
  97.3 0.9 shard_map.57
  (3 shorter events, 0.1 us)
Async XLA Ops:
  0.0 38.8 %copy-start = (bf16[192,512]{1,0:T(8,128)(2,1)S(1)}, bf16[192,512]{1,0:T(8,128)(2,1)}, u32[]{:S(2)}) copy-start(bf16[192,512]{1,0:T(8,128)(2,1)} %source_ref.1) | copy-start | bytes 589828
  0.8 6.1 %collective-permute-start.1 = (f32[2,128]{1,0:T(2,128)S(1)}, f32[2,128]{1,0:T(2,128)S(1)}, u32[]{:S(2)}, u32[]{:S(2)}) collective-permute-start(f32[2,128]{1,0:T(2,128)S(1)} %broadcast_in_dim.2.ids_ref), channel_id=1, source_target_pairs={{0,0},{64,1},{1,8},{65,9},{2,18},{66,19},{3,26},{67,27},{4,36},{68... | collective-permute-start | bytes 3080 | tf_op jit(solution)/shard_map/ppermute | solution.py:286
  6.9 0.7 copy-start.1
  7.6 0.7 copy-start.2
  36.9 12.7 %collective-permute-start.2 = (bf16[2,784,128]{2,1,0:T(8,128)(2,1)S(1)}, bf16[2,784,128]{2,1,0:T(8,128)(2,1)S(1)}, u32[]{:S(2)}, u32[]{:S(2)}) collective-permute-start(bf16[2,784,128]{2,1,0:T(8,128)(2,1)S(1)} %all_gather.3), channel_id=1, source_target_pairs={{0,56},{1,9},{8,0},{9,17},{16,8},{17,25},{24,16},{25,33},{32,24},{... | collective-permute-start | bytes 1204232 | tf_op jit(solution)/shard_map/ppermute | solution.py:267
  38.9 12.7 %collective-permute-start = (bf16[192,512]{1,0:T(8,128)(2,1)S(1)}, bf16[192,512]{1,0:T(8,128)(2,1)S(1)}, u32[]{:S(2)}, u32[]{:S(2)}) collective-permute-start(bf16[192,512]{1,0:T(8,128)(2,1)S(1)} %copy-done), channel_id=1, source_target_pairs={{0,64},{64,0},{1,65},{65,1},{2,66},{66,2},{3,67},{67,3},{4,68},{68... | collective-permute-start | bytes 589832 | tf_op jit(solution)/shard_map/ppermute | solution.py:272
  49.6 9.8 %collective-permute-start.3 = (bf16[2,784,128]{2,1,0:T(8,128)(2,1)S(1)}, bf16[2,784,128]{2,1,0:T(8,128)(2,1)S(1)}, u32[]{:S(2)}, u32[]{:S(2)}) collective-permute-start(bf16[2,784,128]{2,1,0:T(8,128)(2,1)S(1)} %collective-permute-done.2.refs_3_), channel_id=1, source_target_pairs={{0,56},{1,9},{8,0},{9,17},{16,8},{17,25},{24,16},{25,33},{32,24},{... | collective-permute-start | bytes 1204232 | tf_op jit(solution)/shard_map/ppermute | solution.py:267
  51.6 9.7 %collective-permute-start.6 = (bf16[2,784,128]{2,1,0:T(8,128)(2,1)S(1)}, bf16[2,784,128]{2,1,0:T(8,128)(2,1)S(1)}, u32[]{:S(2)}, u32[]{:S(2)}) collective-permute-start(bf16[2,784,128]{2,1,0:T(8,128)(2,1)S(1)} %shard_map.47.refs_0_), channel_id=1, source_target_pairs={{0,1},{1,0},{2,3},{3,2},{4,5},{5,4},{6,7},{7,6},{8,9},{9,8},{10,11... | collective-permute-start | bytes 1204232 | tf_op jit(solution)/shard_map/ppermute | solution.py:272
  59.4 11.3 %collective-permute-start.4 = (bf16[2,784,128]{2,1,0:T(8,128)(2,1)S(1)}, bf16[2,784,128]{2,1,0:T(8,128)(2,1)S(1)}, u32[]{:S(2)}, u32[]{:S(2)}) collective-permute-start(bf16[2,784,128]{2,1,0:T(8,128)(2,1)S(1)} %collective-permute-done.3.refs_2_), channel_id=1, source_target_pairs={{0,56},{1,9},{8,0},{9,17},{16,8},{17,25},{24,16},{25,33},{32,24},{... | collective-permute-start | bytes 1204232 | tf_op jit(solution)/shard_map/ppermute | solution.py:267
  70.8 7.7 %collective-permute-start.5 = (bf16[1,784,128]{2,1,0:T(8,128)(2,1)S(1)}, bf16[1,784,128]{2,1,0:T(8,128)(2,1)S(1)}, u32[]{:S(2)}, u32[]{:S(2)}) collective-permute-start(bf16[1,784,128]{2,1,0:T(8,128)(2,1)S(1)} %shard_map.50), channel_id=1, source_target_pairs={{0,56},{1,9},{8,0},{9,17},{16,8},{17,25},{24,16},{25,33},{32,24},{... | collective-permute-start | bytes 602120 | tf_op jit(solution)/shard_map/ppermute | solution.py:267
  79.7 8.9 %collective-permute-start.7 = (bf16[2,144,768]{2,1,0:T(8,128)(2,1)S(1)}, bf16[2,144,768]{2,1,0:T(8,128)(2,1)S(1)}, u32[]{:S(2)}, u32[]{:S(2)}) collective-permute-start(bf16[2,144,768]{2,1,0:T(8,128)(2,1)S(1)} %shard_map.55), channel_id=1, source_target_pairs={{0,1},{1,0},{2,3},{3,2},{4,5},{5,4},{6,7},{7,6},{8,9},{9,8},{10,11... | collective-permute-start | bytes 1327112 | tf_op jit(solution)/shard_map/ppermute | solution.py:272
  88.7 8.5 %collective-permute-start.8 = (bf16[2,144,384]{2,1,0:T(8,128)(2,1)S(1)}, bf16[2,144,384]{2,1,0:T(8,128)(2,1)S(1)}, u32[]{:S(2)}, u32[]{:S(2)}) collective-permute-start(bf16[2,144,384]{2,1,0:T(8,128)(2,1)S(1)} %get-tuple-element.8), channel_id=1, source_target_pairs={{0,64},{64,0},{1,65},{65,1},{2,66},{66,2},{3,67},{67,3},{4,68},{68... | collective-permute-start | bytes 663560 | tf_op jit(solution)/shard_map/ppermute | solution.py:272
